TPU v7x, 128 devices: a whole 4x4x4 slice. The times are simulated.
128 devices in a mesh: op: 4 (over z), row: 32 (over y, x, core).
Axes of the slice: x: 4, y: 4, z: 4, core: 2. Of those that a mesh axis runs over, the one named last changes fastest.
Arguments:
- wannier_ops: bfloat16 [2, 4000, 2, 128, 128], P(None, 'row'), may hold values from -0.09375 to 0.09375
- r_coords: int32 [4000, 3], P('row'), may hold values from -8 to 8
- degeneracy: int32 [4000], P('row'), may hold values from 1 to 4
- kpoints: int32 [256, 3], replicated, may hold values from 0 to 15
- bloch_vectors: bfloat16 [256, 2, 64, 128], P(('op', 'row')), may hold values from -0.375 to 0.375
Outputs:
- covariant: float32 [256, 2, 4096], P(('op', 'row'))
Inputs may be any that keep to these rules, and one draw needn't show every extreme that they name: `r_coords`: these coordinates are small integers; a program may pack several of them into one int32 word when it moves them. `degeneracy`: these degeneracies are small integers; a program may pack several of them into one int32 word when it moves them.
All inputs are finite; a program needn't handle non-finite values.
Results may differ from a plain program's by a relative error of at most 0.0038.
Values may be sent and summed in bfloat16 or wider, within the bound.
No kernel may reach another device: no remote copies, remote signals or barrier semaphores. Data moves between devices by JAX's collectives and lax.ppermute only.
A program may use at most 192 MiB of HBM per device.

v0:
```python
import math

import jax
import jax.numpy as jnp
from jax import lax
from jax.sharding import PartitionSpec as P

GRID = 16
RMAX = 8


TWO_PI = 6.283185307179586
HIGH = lax.Precision.HIGHEST


def in_one_piece(arrays, axis, dim, along):
    widths = [math.prod(a.shape[along:]) for a in arrays]
    both = jnp.concatenate(
        [a.reshape(*a.shape[:along], w) for a, w in zip(arrays, widths)], axis=along
    )
    whole = lax.all_gather(both, axis, axis=dim, tiled=True)
    parts = jnp.split(whole, [sum(widths[:k]) for k in range(1, len(widths))], axis=along)
    return tuple((b.reshape(*whole.shape[:along], *a.shape[along:]) for a, b in zip(arrays, parts)))


def split_up(x, dim, peers):
    before, after = (x.shape[:dim], x.shape[dim + 1 :])
    return jnp.moveaxis(x.reshape(*before, peers, -1, *after), dim, 0)


def piece_ends(length, count):
    step = length // count
    if step >= 8:
        step -= step % 8
    return [step * k for k in range(1, count)]


def joined_along(parts, dim):
    parts = jnp.moveaxis(parts, 0, dim)
    shape = parts.shape
    return parts.reshape(*shape[:dim], shape[dim] * shape[dim + 1], *shape[dim + 2 :])


def several_exchanges(x, axis, pieces, split_dim, concat_dim):
    parts = split_up(x, split_dim, lax.axis_size(axis))
    widest = max(range(1, max(2, parts.ndim - 1)), key=lambda d: parts.shape[d])
    gathered = []
    for section in jnp.split(parts, piece_ends(parts.shape[widest], pieces), axis=widest):
        if section.size:
            gathered.append(lax.all_to_all(section, axis, split_axis=0, concat_axis=0, tiled=True))
    return joined_along(jnp.concatenate(gathered, axis=widest), concat_dim)


def phase_parts(r_coords, degeneracy, kpoints):
    turns_int = jnp.sum(r_coords[:, None, :] * kpoints[None, :, :], axis=2) % GRID
    angles = turns_int.astype(jnp.float32) * (TWO_PI / GRID)
    weights = 1.0 / degeneracy.astype(jnp.float32)
    cosine = jnp.cos(angles) * weights[:, None]
    sine_part = jnp.sin(angles) * weights[:, None]
    along_x = (r_coords[:, 0].astype(jnp.float32) / RMAX)[:, None]
    return (cosine, sine_part, along_x)


def fourier(phase_re, phase_im, flat_ops):
    stacked = jnp.concatenate([phase_re, phase_im], axis=1)
    product_sum = lax.dot_general(
        stacked, flat_ops, (((0,), (0,)), ((), ())), preferred_element_type=jnp.float32
    )
    k_count = phase_re.shape[1]
    half_cols = flat_ops.shape[1] // 2
    real_part = product_sum[:k_count, :half_cols] - product_sum[k_count:, half_cols:]
    imag_part = product_sum[:k_count, half_cols:] + product_sum[k_count:, :half_cols]
    return (real_part, imag_part)


def complex_mul(form, left, right):

    def single(first, second):
        return jnp.einsum(form, first, second, precision=HIGH)

    return (
        single(left[0], right[0]) - single(left[1], right[1]),
        single(left[0], right[1]) + single(left[1], right[0]),
    )


def rotate(op_pair, vec_pair):
    left_side = complex_mul("knm,kmp->knp", (vec_pair[0], -vec_pair[1]), op_pair)
    return complex_mul("knm,kpm->knp", left_side, vec_pair)


def covariant_form(ham, deriv, posit, posit_deriv):
    band_count = ham[0].shape[-1]
    factor = 1.0 / math.sqrt(band_count)
    form = "kab,kbc->kac"
    a_d = complex_mul(form, posit, deriv)
    d_a = complex_mul(form, deriv, posit)
    h_a = complex_mul(form, ham, posit)
    a_h = complex_mul(form, posit, ham)
    g_real = posit_deriv[0] + factor * (h_a[0] + a_h[0] - (a_d[1] - d_a[1]))
    g_imag = posit_deriv[1] + factor * (h_a[1] + a_h[1] + (a_d[0] - d_a[0]))
    k_count = g_real.shape[0]
    return jnp.stack([g_real.reshape(k_count, -1), g_imag.reshape(k_count, -1)], axis=1)


def make_phases(coords, degens, kpoints, derive):
    cosine, sine_part, along_x = phase_parts(coords, degens, kpoints)
    phase_re = jnp.where(derive, -along_x * sine_part, cosine).astype(jnp.bfloat16)
    phase_im = jnp.where(derive, along_x * cosine, sine_part).astype(jnp.bfloat16)
    return (phase_re, phase_im)


def on_device(wannier_ops, r_coords, degeneracy, kpoints, bloch_vectors):
    row_count = lax.axis_size("row")
    op_count = lax.axis_size("op")
    component = lax.axis_index("op")
    base_ops = lax.dynamic_index_in_dim(wannier_ops, component // 2, 0, keepdims=False)
    r_local = base_ops.shape[0]
    width = base_ops.shape[-1]
    derive = component % 2 == 1
    total_k = kpoints.shape[0]
    per_block = total_k // (row_count * op_count)
    vectors = bloch_vectors.astype(jnp.float32)
    vec_pair = (vectors[:, 0], vectors[:, 1])
    every_coords, every_degen = in_one_piece((r_coords, degeneracy), "row", 0, 1)
    phase_re, phase_im = make_phases(every_coords, every_degen, kpoints, derive)
    entry_ops = base_ops.reshape(r_local, 2, width * width)
    moved = several_exchanges(entry_ops, "row", 2, 2, 0)
    all_r = moved.shape[0]
    slice_cols = moved.shape[2]
    real_part, imag_part = fourier(phase_re, phase_im, moved.reshape(all_r, 2 * slice_cols))
    local_sums = jnp.stack([real_part, imag_part], axis=1)[None]
    owned = lax.all_to_all(local_sums, ("op", "row"), split_axis=1, concat_axis=0, tiled=True)
    owned = owned.reshape(op_count, row_count, per_block, 2, slice_cols)
    owned = jnp.transpose(owned, (0, 2, 3, 1, 4)).reshape(op_count, per_block, 2, width * width)
    rotated = []
    for component_id in range(4):
        op_pair = (
            owned[component_id, :, 0].reshape(per_block, width, width),
            owned[component_id, :, 1].reshape(per_block, width, width),
        )
        rotated.append(rotate(op_pair, vec_pair))
    return covariant_form(rotated[0], rotated[1], rotated[2], rotated[3])


def solution(mesh):
    in_specs = (
        P(None, "row", None, None, None),
        P("row", None),
        P("row"),
        P(),
        P(("op", "row"), None, None, None),
    )
    out_specs = P(("op", "row"), None, None)
    return jax.shard_map(
        on_device, mesh=mesh, in_specs=in_specs, out_specs=out_specs, check_vma=False
    )
```

profile of v0, /device:TPU:24, one launch (start us, length us, event | category | flops | bytes accessed | tf_op | source)
XLA Modules:
  0.0 261.7 jit_solution(8764710877351975365)
XLA Ops:
  0.0 10.1 %constant_dynamic-slice_fusion = bf16[1,125,2,128,128]{4,3,2,1,0:T(8,128)(2,1)} fusion(bf16[2,125,2,128,128]{4,3,2,1,0:T(8,128)(2,1)} %param.5, s32[]{:T(128)S(6)} %select_n.39), kind=kLoop, calls=%fused_computation.119 | loop fusion | bytes 16384004 | tf_op jit(solution)/shard_map/jit(dynamic_index_in_dim)/dynamic_slice | solution.py:117
  10.1 12.5 %copy.44 = bf16[1,125,2,128,128]{1,4,3,2,0:T(8,128)(2,1)} copy(bf16[1,125,2,128,128]{4,3,2,1,0:T(8,128)(2,1)} %constant_dynamic-slice_fusion) | data formatting | bytes 16384000 | tf_op jit(solution)/shard_map/jit(dynamic_index_in_dim)/dynamic_slice | solution.py:117
  22.7 8.4 %copy.45 = bf16[32,56,2,512]{3,1,2,0:T(8,128)(2,1)} copy(bf16[32,56,2,512]{1,3,0,2:T(8,128)(2,1)} %bitcast.204) | data formatting | bytes 7340032 | tf_op jit(solution)/shard_map/split | solution.py:48
  31.1 7.4 %all-to-all-start = ((bf16[32,56,2,512]{3,1,2,0:T(8,128)(2,1)}), bf16[32,56,2,512]{3,1,2,0:T(8,128)(2,1)}, u32[]{:S(2)}, u32[]{:S(2)}) async-start(bf16[32,56,2,512]{3,1,2,0:T(8,128)(2,1)} %copy.45), calls=%async_computation | async-start | bytes 7340032 | tf_op jit(solution)/shard_map/all_to_all | solution.py:50
  38.5 9.0 %split.19 = bf16[32,69,2,512]{1,3,0,2:T(8,128)(2,1)} slice(bf16[32,125,2,512]{1,3,0,2:T(8,128)(2,1)} %bitcast.205), slice={[0:32], [56:125], [0:2], [0:512]} | slice | bytes 9043968 | tf_op jit(solution)/shard_map/split | solution.py:48
  47.5 15.1 %copy.46 = bf16[32,69,2,512]{3,2,1,0:T(2,128)(2,1)} copy(bf16[32,69,2,512]{1,3,0,2:T(8,128)(2,1)} %split.19) | data formatting | bytes 9043968 | tf_op jit(solution)/shard_map/split | solution.py:48
  62.7 21.1 %all-to-all-done = bf16[32,56,2,512]{3,1,2,0:T(8,128)(2,1)} async-done(((bf16[32,56,2,512]{3,1,2,0:T(8,128)(2,1)}), bf16[32,56,2,512]{3,1,2,0:T(8,128)(2,1)}, u32[]{:S(2)}, u32[]{:S(2)}) %all-to-all-start) | async-done | bytes 3670048 | tf_op jit(solution)/shard_map/all_to_all | solution.py:50
  83.7 7.5 %all-to-all-start.1 = ((bf16[32,69,2,512]{3,2,1,0:T(2,128)(2,1)}), bf16[32,69,2,512]{3,2,1,0:T(2,128)(2,1)}, u32[]{:S(2)}, u32[]{:S(2)}) async-start(bf16[32,69,2,512]{3,2,1,0:T(2,128)(2,1)} %copy.46), calls=%async_computation.1 | async-start | bytes 9043968 | tf_op jit(solution)/shard_map/all_to_all | solution.py:50
  91.3 71.3 %all-gather = s32[32,125,4]{1,2,0:T(4,128)S(1)} all-gather(s32[1,125,4]{1,2,0:T(4,128)S(1)} %add_bitcast_fusion), channel_id=1, replica_groups=mesh['op'=4,'row'=32] {'row'}, dimensions={0}, use_global_device_ids=true | all-gather | bytes 66000 | tf_op jit(solution)/shard_map/all_gather | solution.py:21
  162.8 5.1 %multiply_reduce_fusion = s32[4000,256]{1,0:T(8,128)S(1)} fusion(s32[256,3]{0,1:T(4,128)S(1)} %copy-done.1, s32[4000,3]{0,1:T(4,128)S(1)} %bitcast.226), kind=kLoop, calls=%fused_computation | loop fusion | flops 5120000 | bytes 4147072 | tf_op jit(solution)/shard_map/reduce_sum | solution.py:55
  167.9 20.3 %select_convert_fusion.1 = (bf16[4000,256]{1,0:T(8,128)(2,1)}, bf16[4000,256]{1,0:T(8,128)(2,1)}) fusion(f32[4000]{0:T(1024)S(1)} %bitcast.228, f32[4000]{0:T(1024)S(1)} %bitcast.227, pred[]{:T(512)S(6)} %eq.7, s32[4000,256]{1,0:T(8,128)S(1)} %multiply_reduce_fusion, f32[4000]{0:T(1024)S(1)} %bitcast.229), kind=kLoop, calls=%fused_computation.13 | loop fusion | flops 21504000 | bytes 8240001 | tf_op jit(solution)/shard_map/convert_element_type | solution.py:108
  188.2 7.5 %copy.47 = bf16[32,56,2,512]{3,2,1,0:T(2,128)(2,1)} copy(bf16[32,56,2,512]{3,1,2,0:T(8,128)(2,1)} %all-to-all-done) | data formatting | bytes 7340032 | tf_op jit(solution)/shard_map/all_to_all | solution.py:50
  195.7 12.2 %pad_maximum_fusion = bf16[32,125,2,512]{3,2,1,0:T(2,128)(2,1)S(1)} fusion(bf16[32,69,2,512]{3,2,1,0:T(2,128)(2,1)} %all-to-all-done.1, bf16[32,56,2,512]{3,2,1,0:T(2,128)(2,1)} %copy.47), kind=kLoop, calls=%fused_computation.1 | loop fusion | flops 4096000 | bytes 16384000 | tf_op jit(solution)/shard_map/concatenate | solution.py:51
  207.9 5.8 %copy.58 = bf16[500,8,2,512]{3,1,2,0:T(8,128)(2,1)} copy(bf16[500,8,2,512]{3,2,1,0:T(2,128)(2,1)S(1)} %bitcast.206) | data formatting | bytes 16384000
  213.7 8.2 %fusion.3 = f32[512,1024]{1,0:T(8,128)S(1)} fusion(bf16[4000,1024]{1,0:T(8,128)(2,1)} %bitcast.207, bf16[4000,256]{1,0:T(8,128)(2,1)} %get-tuple-element.6, bf16[4000,256]{1,0:T(8,128)(2,1)} %get-tuple-element.5), kind=kOutput, calls=%fused_computation.8 | convolution fusion | flops 4202496000 | bytes 14385152 | tf_op jit(solution)/shard_map/dot_general | solution.py:66
  221.9 0.2 fusion.18
  222.2 0.8 copy.49
  223.0 25.8 %all_to_all.19 = f32[1,256,2,512]{3,2,0,1:T(2,128)S(1)} all-to-all(f32[1,256,2,512]{3,2,0,1:T(2,128)S(1)} %copy.49), channel_id=1, replica_groups=mesh['op'=4,'row'=32] {'op','row'}, dimensions={1} | all-to-all | bytes 2097152 | tf_op jit(solution)/shard_map/all_to_all | solution.py:133
  248.8 0.3 copy.60
  249.1 0.9 reshape.21
  250.0 1.0 fusion.111
  251.1 0.2 fusion.51
  251.3 0.2 fusion.53
  251.5 0.2 convolution_subtract_fusion.3
  251.9 0.2 fusion.30
  252.1 0.2 fusion.57
  252.3 0.2 fusion.61
  252.5 0.2 convolution_subtract_fusion.7
  252.9 0.2 fusion.59
  253.1 0.2 convolution_add_fusion.9
  253.3 0.2 fusion.63
  253.5 0.2 fusion.67
  253.7 0.2 convolution_add_fusion.10
  254.0 0.2 convolution_subtract_fusion.9
  254.4 0.2 convolution_subtract_fusion.6
  254.6 0.2 convolution_subtract_fusion.8
  254.8 0.2 fusion.113
  255.0 0.2 fusion.112
  255.4 0.2 fusion.69
  255.6 0.2 fusion.73
  255.8 0.2 convolution_subtract_fusion.11
  256.4 0.2 convolution_add_fusion.6
  256.6 0.2 convolution_subtract_fusion.2
  256.8 0.2 fusion.119
  257.0 0.2 fusion.118
  257.2 0.2 convolution_add_fusion.7
  257.4 0.2 fusion.115
  257.6 0.2 fusion.116
  257.8 0.2 convolution_add_fusion.5
  258.0 0.2 fusion.114
  258.2 0.2 convolution_add_fusion.4
  258.4 0.2 convolution_add_fusion.8
  258.6 0.2 fusion.117
  258.8 0.2 convolution_subtract_fusion.5
  259.0 0.2 convolution_add_fusion.11
  259.2 0.2 fusion.13
  259.4 0.2 fusion.15
  259.6 0.2 fusion.14
  259.9 0.2 convolution_subtract_fusion.1
  260.1 0.2 convolution_add_fusion.1
  260.3 0.2 fusion.9
  260.5 0.2 fusion.16
  260.7 0.2 fusion.10
  261.0 0.7 pad_maximum_fusion.1
  (22 shorter events, 1.5 us)
Async XLA Ops:
  31.1 52.6 %all-to-all-start = ((bf16[32,56,2,512]{3,1,2,0:T(8,128)(2,1)}), bf16[32,56,2,512]{3,1,2,0:T(8,128)(2,1)}, u32[]{:S(2)}, u32[]{:S(2)}) async-start(bf16[32,56,2,512]{3,1,2,0:T(8,128)(2,1)} %copy.45), calls=%async_computation | async-start | bytes 7340032 | tf_op jit(solution)/shard_map/all_to_all | solution.py:50
  62.6 28.6 %copy-start.2 = (s32[125,3]{0,1:T(4,128)S(1)}, s32[125,3]{0,1:T(4,128)}, u32[]{:S(2)}) copy-start(s32[125,3]{0,1:T(4,128)} %param.6) | copy-start | bytes 4504
  62.7 28.7 %copy-start.3 = (s32[125]{0:T(128)S(1)}, s32[125]{0:T(128)}, u32[]{:S(2)}) copy-start(s32[125]{0:T(128)} %param.7) | copy-start | bytes 1504
  62.7 100.1 %copy-start.1 = (s32[256,3]{0,1:T(4,128)S(1)}, s32[256,3]{0,1:T(4,128)}, u32[]{:S(2)}) copy-start(s32[256,3]{0,1:T(4,128)} %param.8) | copy-start | bytes 9220
  83.7 112.0 %all-to-all-start.1 = ((bf16[32,69,2,512]{3,2,1,0:T(2,128)(2,1)}), bf16[32,69,2,512]{3,2,1,0:T(2,128)(2,1)}, u32[]{:S(2)}, u32[]{:S(2)}) async-start(bf16[32,69,2,512]{3,2,1,0:T(2,128)(2,1)} %copy.46), calls=%async_computation.1 | async-start | bytes 9043968 | tf_op jit(solution)/shard_map/all_to_all | solution.py:50
  223.0 28.0 %copy-start = (bf16[2,2,64,128]{3,2,1,0:T(8,128)(2,1)S(1)}, bf16[2,2,64,128]{3,2,1,0:T(8,128)(2,1)}, u32[]{:S(2)}) copy-start(bf16[2,2,64,128]{3,2,1,0:T(8,128)(2,1)} %param.9) | copy-start | bytes 196612
where the time goes:
time: 266 us; the launch traced here: 262 us
  blocking collectives  97.1 us (37%)
  local copies, waits for them, and re-layouts  71.9 us (27%)
  other arithmetic  38.6 us (15%)
  waiting for transfers between devices  21.1 us (8%)
  matrix products  17.5 us (7%)
  starting transfers between devices  14.9 us (6%)
    all_gather x1, blocking collectives, in_one_piece(): whole = lax.all_gather(both, axis, axis=dim, tiled=True)  71.3 us
    split x3, local copies, waits for them, and re-layouts, several_exchanges(): jnp.split(parts, piece_ends(parts.shape[widest], pieces), axis=widest)  32.6 us
    all_to_all x1, blocking collectives, on_device(): lax.all_to_all(local_sums, ('op', 'row'), split_axis=1, concat_axis=0, ti...  25.8 us
    dynamic_slice x2, local copies, waits for them, and re-layouts, on_device(): lax.dynamic_index_in_dim(wannier_ops, component // 2, 0, keepdims=False)  22.7 us
    all_to_all x2, waiting for transfers between devices, several_exchanges(): lax.all_to_all(section, axis, split_axis=0, concat_axis=0, tiled=True)  21.1 us
    convert_element_type x1, other arithmetic, make_phases(): jnp.where(derive, -along_x * sine_part, cosine).astype(jnp.bfloat16)  20.3 us
    all_to_all x2, starting transfers between devices, several_exchanges(): lax.all_to_all(section, axis, split_axis=0, concat_axis=0, tiled=True)  14.9 us
    concatenate x1, other arithmetic, several_exchanges(): return joined_along(jnp.concatenate(gathered, axis=widest), concat_dim)  12.2 us
  transfers between devices with their start and end apart: 2, of which 1 were waited for; matrix products, arithmetic and copies ran while one was open for 22% of the time, Pallas kernels for 0%

commit v1 on v0

v1 whole, which is shorter than its diff:
```python
import functools
import math

import jax
import jax.numpy as jnp
from jax import lax
from jax.experimental import pallas as pl
from jax.experimental.pallas import tpu as pltpu
from jax.sharding import Mesh
from jax.sharding import PartitionSpec as P

GRID = 16
RMAX = 8
TWO_PI = 6.283185307179586
PLANE = ("y", "x", "c")
WHOLE = ("z", "y", "x", "c")
LINK = jnp.bfloat16
SIDE = 4
ROWS = 128


def owner_order(first, y, x, owner_core):
    s1 = jnp.arange(SIDE, dtype=jnp.int32)[:, None]
    s2 = jnp.arange(SIDE, dtype=jnp.int32)[None, :]
    y_step = jnp.where(owner_core == 0, s1, s2)
    x_step = jnp.where(owner_core == 0, s2, s1)
    return (((y + y_step) % SIDE) * SIDE + (x + x_step) % SIDE).reshape(-1)


def phase_matrix(r_coords, degeneracy, kpts):
    count = r_coords.shape[0]
    pad = ROWS - count
    coords = jnp.pad(r_coords, ((0, pad), (0, 0)))
    turns = jnp.sum(kpts[:, None, :] * coords[None, :, :], axis=2) & (GRID - 1)
    angles = turns.astype(jnp.float32) * (TWO_PI / GRID)
    weights = jnp.pad(1.0 / degeneracy.astype(jnp.float32), (0, pad))
    cosine = jnp.cos(angles) * weights[None, :]
    sine = jnp.sin(angles) * weights[None, :]
    along_x = (coords[:, 0].astype(jnp.float32) / RMAX)[None, :]
    re = jnp.stack([cosine, -along_x * sine], axis=1)
    im = jnp.stack([sine, along_x * cosine], axis=1)
    upper = jnp.concatenate([re, -im], axis=2)
    lower = jnp.concatenate([im, re], axis=2)
    full = jnp.stack([upper, lower], axis=2)
    return full.reshape(-1, 2 * ROWS).astype(jnp.bfloat16)


def fourier_body(rows, l_ref, o_ref, f_ref):
    count = o_ref.shape[1]
    halves = []
    for part in range(2):
        block = o_ref[0, :, part]
        block = jnp.concatenate([block, jnp.zeros((ROWS - count, rows, 128), jnp.bfloat16)], axis=0)
        halves.append(jnp.swapaxes(block, 0, 1))
    stacked = jnp.concatenate(halves, axis=1)
    left = l_ref[...]
    sums = []
    for pair in range(rows // 2):
        right = jnp.concatenate([stacked[2 * pair], stacked[2 * pair + 1]], axis=1)
        both = jnp.dot(left, right, preferred_element_type=jnp.float32).astype(f_ref.dtype)
        sums += [both[:, :128], both[:, 128:]]
    f_ref[0] = jnp.swapaxes(jnp.stack(sums, axis=0), 0, 1)


def fourier(phases, ops, rows=16):
    n_ops, count, _, width, _ = ops.shape
    lines = phases.shape[0]
    return pl.pallas_call(
        functools.partial(fourier_body, rows),
        grid=(n_ops, width // rows),
        in_specs=[
            pl.BlockSpec(phases.shape, lambda o, m: (0, 0)),
            pl.BlockSpec((1, count, 2, rows, width), lambda o, m: (o, 0, 0, m, 0)),
        ],
        out_specs=pl.BlockSpec((1, lines, rows, width), lambda o, m: (o, 0, m, 0)),
        out_shape=jax.ShapeDtypeStruct((n_ops, lines, width, width), jnp.bfloat16),
        compiler_params=pltpu.CompilerParams(
            dimension_semantics=("arbitrary", "arbitrary"), vmem_limit_bytes=48 << 20
        ),
        cost_estimate=pl.CostEstimate(flops=4_000_000_000, bytes_accessed=33_000_000, transcendentals=0),
        name="fourier",
    )(phases, ops)


def rotate_body(per_step, half, index_ref, v_ref, f_ref, b_ref):
    step = pl.program_id(0)
    for j in range(per_step):
        where = index_ref[step * per_step + j]
        v_re, v_im = v_ref[where, 0], v_ref[where, 1]
        right = jnp.concatenate(
            [jnp.concatenate([v_re, -v_im], axis=1), jnp.concatenate([v_im, v_re], axis=1)], axis=0
        )
        lines = [
            jnp.concatenate([f_ref[o, j, 2 * p], f_ref[o, j, 2 * p + 1]], axis=1)
            for o in range(2)
            for p in range(2)
        ]
        left = jnp.concatenate(lines, axis=0)
        mid = lax.dot_general(left, right, (((1,), (1,)), ((), ())), preferred_element_type=jnp.float32)
        high = mid.astype(jnp.bfloat16)
        low = (mid - high.astype(jnp.float32)).astype(jnp.bfloat16)
        twice = jnp.concatenate([v_re, v_im], axis=0)
        twice = jnp.concatenate([twice, twice], axis=1)
        lane = lax.broadcasted_iota(jnp.int32, (64, 128), 1)
        sign = jnp.where(lane < 64, 1.0, -1.0)
        for o in range(2):
            cols = []
            for p in range(2):
                at = (2 * o + p) * 128
                cols.append(jnp.concatenate([high[at : at + 128], low[at : at + 128]], axis=0))
            both = jnp.dot(twice, jnp.concatenate(cols, axis=1), preferred_element_type=jnp.float32)
            for p in range(2):
                tile = both[:, 128 * p : 128 * p + 128]
                b_ref[j, 2 * o + p] = tile[:64] + sign * pltpu.roll(tile[64:], 64, 1)


def rotate(index, vectors, sums, half, per_step=4):
    count = index.shape[0]
    first = half * count // per_step
    return pl.pallas_call(
        functools.partial(rotate_body, per_step, half),
        grid_spec=pltpu.PrefetchScalarGridSpec(
            num_scalar_prefetch=1,
            grid=(count // per_step,),
            in_specs=[
                pl.BlockSpec(vectors.shape, lambda g, idx: (0, 0, 0, 0)),
                pl.BlockSpec((2, per_step, 4, 128, 128), lambda g, idx: (0, first + g, 0, 0, 0)),
            ],
            out_specs=pl.BlockSpec((per_step, 4, 64, 128), lambda g, idx: (g, 0, 0, 0)),
        ),
        out_shape=jax.ShapeDtypeStruct((count, 4, 64, 128), jnp.float32),
        compiler_params=pltpu.CompilerParams(
            dimension_semantics=("arbitrary",), vmem_limit_bytes=48 << 20
        ),
        cost_estimate=pl.CostEstimate(flops=2_000_000_000, bytes_accessed=13_000_000, transcendentals=0),
        name="rotate",
    )(index, vectors, sums)


def final_body(b_ref, o_ref):
    factor = 1.0 / math.sqrt(64)
    high = lax.Precision.HIGHEST

    def wide(re, im):
        return jnp.concatenate(
            [jnp.concatenate([re, im], axis=1), jnp.concatenate([-im, re], axis=1)], axis=0
        )

    for k in range(b_ref.shape[0]):
        ham, deriv, posit, extra = (b_ref[k, j] for j in range(4))
        h_re, h_im = ham[:, :64], ham[:, 64:]
        d_re, d_im = deriv[:, :64], deriv[:, 64:]
        p_re, p_im = posit[:, :64], posit[:, 64:]
        one = jnp.dot(posit, wide(h_re - d_im, h_im + d_re), preferred_element_type=jnp.float32, precision=high)
        second = jnp.concatenate([h_re + d_im, h_im - d_re], axis=1)
        two = jnp.dot(second, wide(p_re, p_im), preferred_element_type=jnp.float32, precision=high)
        o_ref[k] = extra + factor * (one + two)


def final(bands):
    return pl.pallas_call(
        final_body,
        out_shape=jax.ShapeDtypeStruct((bands.shape[0], 64, 128), jnp.float32),
        name="final",
    )(bands)


def shift_pairs(stage, shift):
    pairs = []
    for z in range(4):
        for y in range(SIDE):
            for x in range(SIDE):
                for c in range(2):
                    along_y = (c == 0) == (stage == 0)
                    y_to, x_to = ((y + shift) % SIDE, x) if along_y else (y, (x + shift) % SIDE)
                    at = ((z * SIDE + y) * SIDE + x) * 2 + c
                    to = ((z * SIDE + y_to) * SIDE + x_to) * 2 + c
                    pairs.append((at, to))
    return pairs


def on_device(wannier_ops, r_coords, degeneracy, kpoints, bloch_vectors):
    z, y, x, c = (lax.axis_index(name) for name in WHOLE)
    slots = bloch_vectors.shape[0]
    swap = [(0, 1), (1, 0)]
    orders = [owner_order(None, y, x, c), owner_order(None, y, x, 1 - c)]
    slot = jnp.arange(slots, dtype=jnp.int32)
    picks = [(order[:, None] * slots + slot[None, :]).reshape(-1) for order in orders]
    per_plane = 2 * SIDE * SIDE * slots
    owned = []
    for order, core in zip(orders, (c, 1 - c)):
        owned.append((z * per_plane + (order[:, None] * 2 + core) * slots + slot[None, :]).reshape(-1))
    kpts = jnp.take(kpoints, jnp.concatenate(owned), axis=0)

    copies = jnp.broadcast_to(bloch_vectors[None], (SIDE * SIDE, *bloch_vectors.shape))
    mine = lax.all_to_all(copies, ("y", "x"), 0, 0, tiled=True)
    mine = mine.reshape(SIDE * SIDE * slots, 2, 64, 128)
    theirs = lax.ppermute(mine, "c", swap)

    phases = phase_matrix(r_coords, degeneracy, kpts)
    sums = fourier(phases, wannier_ops)
    sums = sums.reshape(2, per_plane, 4, 128, 128)

    bands_mine = rotate(picks[0], mine, sums, 0)
    bands_theirs = rotate(picks[1], theirs, sums, 1)
    bands_mine = bands_mine + lax.ppermute(bands_theirs, "c", swap)

    parts = bands_mine.reshape(SIDE, -1, 4, 64, 128)
    total = parts[0]
    for got in [lax.ppermute(parts[s].astype(LINK), WHOLE, shift_pairs(0, s)) for s in (1, 2, 3)]:
        total = total + got.astype(jnp.float32)
    parts = total.reshape(SIDE, slots, 4, 64, 128)
    total = parts[0]
    for got in [lax.ppermute(parts[s], WHOLE, shift_pairs(1, s)) for s in (1, 2, 3)]:
        total = total + got
    out = final(total)
    out = out.reshape(slots, 64, 2, 64)
    return jnp.transpose(out, (0, 2, 1, 3)).reshape(slots, 2, 64 * 64)


def solution(mesh):
    torus = Mesh(mesh.devices.reshape(4, 4, 4, 2), WHOLE)
    in_specs = (
        P(None, PLANE, None, None, None),
        P(PLANE, None),
        P(PLANE),
        P(),
        P(WHOLE, None, None, None),
    )
    return jax.shard_map(
        on_device, mesh=torus, in_specs=in_specs, out_specs=P(WHOLE, None, None), check_vma=False
    )
```

time: 266 us -> 116 us (0.44); the launches traced: 262 us -> 114 us
  blocking collectives: 97.1 us -> 0 us
  local copies, waits for them, and re-layouts: 71.9 us -> 7.25 us
  Pallas kernels: 0 us -> 52.2 us
  other arithmetic: 38.6 us -> 7.84 us
  matrix products: 17.5 us -> 0 us
  waiting for transfers between devices: 21.1 us -> 31.4 us
    all_gather x1 -> x0, blocking collectives: 71.3 us -> none  [in_one_piece(): whole = lax.all_gather(both, axis, axis=dim, tiled=True)]
    pallas_call x0 -> x4, Pallas kernels: none -> 52.2 us  [the longest x2 28 us: rotate(): pl.pallas_call(functools.partial(rotate_body, per_step, half), grid_spec=...]
    split x3 -> x0, local copies, waits for them, and re-layouts: 32.6 us -> none  [several_exchanges(): jnp.split(parts, piece_ends(parts.shape[widest], pieces), axis=widest)]
    all_to_all x1 -> x0, blocking collectives: 25.8 us -> none  [on_device(): lax.all_to_all(local_sums, ('op', 'row'), split_axis=1, concat_axis=0, ti...]
    dynamic_slice x2 -> x0, local copies, waits for them, and re-layouts: 22.7 us -> none  [on_device(): lax.dynamic_index_in_dim(wannier_ops, component // 2, 0, keepdims=False)]
    ppermute x0 -> x8, waiting for transfers between devices: none -> 22.3 us  [the longest x3 14.5 us: on_device(): lax.ppermute(parts[s].astype(LINK), WHOLE, shift_pairs(0, s))]
    convert_element_type x1 -> x0, other arithmetic: 20.3 us -> none  [make_phases(): jnp.where(derive, -along_x * sine_part, cosine).astype(jnp.bfloat16)]
    dot_general x49 -> x0, matrix products: 17.5 us -> none  [the longest x48 9.37 us: single(): return jnp.einsum(form, first, second, precision=HIGH)]
  transfers between devices with their start and end apart: 2 -> 9, of which waited for: 1 -> 6; matrix products, arithmetic and copies ran while one was open for 22% -> 5% of each run, Pallas kernels for 0% -> 31%
where the time goes in v1:
time: 116 us; the launch traced here: 114 us
  Pallas kernels  52.2 us (45%)
  waiting for transfers between devices  31.4 us (27%)
  starting transfers between devices  15.5 us (13%)
  other arithmetic  7.84 us (7%)
  local copies, waits for them, and re-layouts  7.25 us (6%)
    pallas_call x2, Pallas kernels, rotate(): pl.pallas_call(functools.partial(rotate_body, per_step, half), grid_spec=...  28 us
    pallas_call x1, Pallas kernels, fourier(): pl.pallas_call(functools.partial(fourier_body, rows), grid=(n_ops, width...  22.2 us
    ppermute x3, waiting for transfers between devices, on_device(): lax.ppermute(parts[s].astype(LINK), WHOLE, shift_pairs(0, s))  14.5 us
    all_to_all x1, waiting for transfers between devices, on_device(): mine = lax.all_to_all(copies, ('y', 'x'), 0, 0, tiled=True)  9.09 us
    ppermute x3, waiting for transfers between devices, on_device(): lax.ppermute(parts[s], WHOLE, shift_pairs(1, s))  7.87 us
    all_to_all x1, starting transfers between devices, on_device(): mine = lax.all_to_all(copies, ('y', 'x'), 0, 0, tiled=True)  7.17 us
    ppermute x3, starting transfers between devices, on_device(): lax.ppermute(parts[s].astype(LINK), WHOLE, shift_pairs(0, s))  4.51 us
    another operation x4, other arithmetic  3.72 us
  transfers between devices with their start and end apart: 9, of which 6 were waited for; matrix products, arithmetic and copies ran while one was open for 5% of the time, Pallas kernels for 31%

profile of v1, /device:TPU:24, one launch (start us, length us, event | category | flops | bytes accessed | tf_op | source)
XLA Modules:
  0.0 114.4 jit_solution(6170670226177821749)
XLA Ops:
  0.0 2.1 %broadcast_in_dim.85 = bf16[16,2,2,64,128]{4,3,2,1,0:T(8,128)(2,1)} broadcast(bf16[2,2,64,128]{3,2,1,0:T(8,128)(2,1)} %param.9), dimensions={1,2,3,4} | broadcast | bytes 1114112 | tf_op jit(solution)/shard_map/broadcast_in_dim | solution.py:195
  2.1 7.2 %all-to-all-start = ((bf16[16,2,2,64,128]{4,3,2,1,0:T(8,128)(2,1)}), bf16[16,2,2,64,128]{4,3,2,1,0:T(8,128)(2,1)S(1)}, u32[]{:S(2)}, u32[]{:S(2)}) async-start(bf16[16,2,2,64,128]{4,3,2,1,0:T(8,128)(2,1)} %broadcast_in_dim.85), calls=%async_computation | async-start | bytes 2097152 | tf_op jit(solution)/shard_map/all_to_all | solution.py:196
  9.3 0.1 add.338
  9.4 0.1 add.341
  9.5 0.1 add.322
  9.6 0.1 add.318
  9.7 0.1 iota_add_fusion.1
  9.7 0.1 concatenate.40
  9.8 0.1 add.350
  9.9 0.1 iota_add_fusion.2
  10.0 0.1 concatenate.39
  10.1 0.1 add.336
  10.2 0.7 pad.8
  10.9 0.1 fusion.13
  10.9 0.8 copy.15
  11.8 0.1 compare_and_fusion
  11.8 0.6 gather_fusion
  12.4 0.1 broadcast_select_fusion
  12.5 0.1 copy.16
  12.6 0.7 convert_divide_fusion
  13.3 0.7 fusion.16
  14.0 0.7 multiply_bitcast_fusion
  14.7 0.1 multiply_reduce_fusion
  14.7 0.1 broadcast_multiply_fusion.1
  14.9 0.1 broadcast_multiply_fusion
  15.0 9.1 %all-to-all-done = bf16[16,2,2,64,128]{4,3,2,1,0:T(8,128)(2,1)S(1)} async-done(((bf16[16,2,2,64,128]{4,3,2,1,0:T(8,128)(2,1)}), bf16[16,2,2,64,128]{4,3,2,1,0:T(8,128)(2,1)S(1)}, u32[]{:S(2)}, u32[]{:S(2)}) %all-to-all-start) | async-done | bytes 1048608 | tf_op jit(solution)/shard_map/all_to_all | solution.py:196
  24.1 0.0 collective-permute-start
  24.1 0.1 iota_add_fusion
  24.2 0.1 add.358.index_ref
  24.4 0.1 copy.18
  24.5 0.1 convert_element_type.57.l_ref
  24.6 22.2 %fourier.1 = bf16[2,256,128,128]{3,2,1,0:T(8,128)(2,1)} custom-call(bf16[256,256]{1,0:T(8,128)(2,1)S(1)} %convert_element_type.57.l_ref, bf16[2,125,2,128,128]{4,3,2,1,0:T(8,128)(2,1)} %o_ref.1), custom_call_target="tpu_custom_call" | custom-call | flops 4000000000 | bytes 33000000 | tf_op jit(solution)/shard_map/fourier/pallas_call | solution.py:68
  46.8 0.0 collective-permute-done.v_ref
  46.8 14.4 %rotate.3 = f32[32,4,64,128]{3,2,1,0:T(8,128)} custom-call(s32[32]{0:T(128)S(1)} %add.358.index_ref, bf16[32,2,64,128]{3,2,1,0:T(8,128)(2,1)S(1)} %collective-permute-done.v_ref, bf16[2,64,4,128,128]{4,3,2,1,0:T(8,128)(2,1)} %bitcast.25), custom_call_target="tpu_custom_call" | custom-call | flops 2000000000 | bytes 13000000 | tf_op jit(solution)/shard_map/rotate/pallas_call | solution.py:120
  61.2 0.5 collective-permute-start.1
  61.7 0.1 iota_add_fusion.3
  61.8 0.1 add.328.index_ref
  61.9 13.6 %rotate.2 = f32[32,4,64,128]{3,2,1,0:T(8,128)S(1)} custom-call(s32[32]{0:T(128)S(1)} %add.328.index_ref, bf16[32,2,64,128]{3,2,1,0:T(8,128)(2,1)S(1)} %bitcast.24, bf16[2,64,4,128,128]{4,3,2,1,0:T(8,128)(2,1)} %bitcast.26), custom_call_target="tpu_custom_call" | custom-call | flops 2000000000 | bytes 13000000 | tf_op jit(solution)/shard_map/rotate/pallas_call | solution.py:120
  75.4 0.0 collective-permute-done.1
  75.5 3.7 %fusion.17 = (bf16[32,4,64,128]{3,2,1,0:T(8,128)(2,1)S(1)}, f32[32,4,64,128]{3,2,1,0:T(8,128)S(1)}) fusion(f32[32,4,64,128]{3,2,1,0:T(8,128)S(1)} %rotate.2, f32[32,4,64,128]{3,2,1,0:T(8,128)} %collective-permute-done.1), kind=kLoop, calls=%fused_computation.61 | loop fusion | flops 2097152 | bytes 14680064 | tf_op jit(solution)/shard_map/convert.2
  79.2 0.2 fusion.20
  79.3 3.0 %collective-permute-start.2 = (bf16[8,4,64,128]{3,2,1,0:T(8,128)(2,1)S(1)}, bf16[8,4,64,128]{3,2,1,0:T(8,128)(2,1)S(1)}, u32[]{:S(2)}, u32[]{:S(2)}) collective-permute-start(bf16[8,4,64,128]{3,2,1,0:T(8,128)(2,1)S(1)} %get-tuple-element.15), channel_id=1, source_target_pairs={{0,8},{1,3},{2,10},{3,5},{4,12},{5,7},{6,14},{7,1},{8,16},{9,11},{... | collective-permute-start | bytes 1572872 | tf_op jit(solution)/shard_map/ppermute | solution.py:210
  82.3 0.0 collective-permute-start.4
  82.3 1.5 %collective-permute-start.3 = (bf16[8,4,64,128]{3,2,1,0:T(8,128)(2,1)S(1)}, bf16[8,4,64,128]{3,2,1,0:T(8,128)(2,1)S(1)}, u32[]{:S(2)}, u32[]{:S(2)}) collective-permute-start(bf16[8,4,64,128]{3,2,1,0:T(8,128)(2,1)S(1)} %get-tuple-element.17), channel_id=1, source_target_pairs={{0,16},{1,5},{2,18},{3,7},{4,20},{5,1},{6,22},{7,3},{8,24},{9,13},... | collective-permute-start | bytes 1572872 | tf_op jit(solution)/shard_map/ppermute | solution.py:210
  83.8 10.8 %collective-permute-done.2 = bf16[8,4,64,128]{3,2,1,0:T(8,128)(2,1)S(1)} collective-permute-done((bf16[8,4,64,128]{3,2,1,0:T(8,128)(2,1)S(1)}, bf16[8,4,64,128]{3,2,1,0:T(8,128)(2,1)S(1)}, u32[]{:S(2)}, u32[]{:S(2)}) %collective-permute-start.2) | collective-permute-done | bytes 524320 | tf_op jit(solution)/shard_map/ppermute | solution.py:210
  94.6 3.7 %collective-permute-done.4 = bf16[8,4,64,128]{3,2,1,0:T(8,128)(2,1)S(1)} collective-permute-done((bf16[8,4,64,128]{3,2,1,0:T(8,128)(2,1)S(1)}, bf16[8,4,64,128]{3,2,1,0:T(8,128)(2,1)S(1)}, u32[]{:S(2)}, u32[]{:S(2)}) %collective-permute-start.4) | collective-permute-done | bytes 524320 | tf_op jit(solution)/shard_map/ppermute | solution.py:210
  98.3 0.0 collective-permute-done.3
  98.3 0.3 fusion.1
  98.7 0.1 fusion.21
  98.7 0.1 collective-permute-start.5
  98.8 3.2 %collective-permute-start.7 = (f32[2,4,64,128]{3,2,1,0:T(8,128)S(1)}, f32[2,4,64,128]{3,2,1,0:T(8,128)S(1)}, u32[]{:S(2)}, u32[]{:S(2)}) collective-permute-start(f32[2,4,64,128]{3,2,1,0:T(8,128)S(1)} %get-tuple-element.19), channel_id=1, source_target_pairs={{0,6},{1,25},{2,0},{3,27},{4,2},{5,29},{6,4},{7,31},{8,14},{9,1},{... | collective-permute-start | bytes 786440 | tf_op jit(solution)/shard_map/ppermute | solution.py:214
  102.0 0.0 collective-permute-start.6
  102.0 4.3 %collective-permute-done.5 = f32[2,4,64,128]{3,2,1,0:T(8,128)S(1)} collective-permute-done((f32[2,4,64,128]{3,2,1,0:T(8,128)S(1)}, f32[2,4,64,128]{3,2,1,0:T(8,128)S(1)}, u32[]{:S(2)}, u32[]{:S(2)}) %collective-permute-start.5) | collective-permute-done | bytes 262176 | tf_op jit(solution)/shard_map/ppermute | solution.py:214
  106.4 2.4 %collective-permute-done.7 = f32[2,4,64,128]{3,2,1,0:T(8,128)S(1)} collective-permute-done((f32[2,4,64,128]{3,2,1,0:T(8,128)S(1)}, f32[2,4,64,128]{3,2,1,0:T(8,128)S(1)}, u32[]{:S(2)}, u32[]{:S(2)}) %collective-permute-start.7) | collective-permute-done | bytes 262176 | tf_op jit(solution)/shard_map/ppermute | solution.py:214
  108.7 1.2 %collective-permute-done.6 = f32[2,4,64,128]{3,2,1,0:T(8,128)S(1)} collective-permute-done((f32[2,4,64,128]{3,2,1,0:T(8,128)S(1)}, f32[2,4,64,128]{3,2,1,0:T(8,128)S(1)}, u32[]{:S(2)}, u32[]{:S(2)}) %collective-permute-start.6) | collective-permute-done | bytes 262176 | tf_op jit(solution)/shard_map/ppermute | solution.py:214
  109.9 0.8 fusion.3.b_ref
  110.7 2.0 %final.1 = f32[2,64,128]{2,1,0:T(8,128)} custom-call(f32[2,4,64,128]{3,2,1,0:T(8,128)} %fusion.3.b_ref), custom_call_target="tpu_custom_call" | custom-call | tf_op jit(solution)/shard_map/final/pallas_call | solution.py:161
  112.7 1.0 reshape.491
  113.7 0.7 reshape.492
  (13 shorter events, 0.1 us)
Async XLA Ops:
  2.1 22.0 %all-to-all-start = ((bf16[16,2,2,64,128]{4,3,2,1,0:T(8,128)(2,1)}), bf16[16,2,2,64,128]{4,3,2,1,0:T(8,128)(2,1)S(1)}, u32[]{:S(2)}, u32[]{:S(2)}) async-start(bf16[16,2,2,64,128]{4,3,2,1,0:T(8,128)(2,1)} %broadcast_in_dim.85), calls=%async_computation | async-start | bytes 2097152 | tf_op jit(solution)/shard_map/all_to_all | solution.py:196
  24.1 22.6 %collective-permute-start = (bf16[32,2,64,128]{3,2,1,0:T(8,128)(2,1)S(1)}, bf16[32,2,64,128]{3,2,1,0:T(8,128)(2,1)S(1)}, u32[]{:S(2)}, u32[]{:S(2)}) collective-permute-start(bf16[32,2,64,128]{3,2,1,0:T(8,128)(2,1)S(1)} %bitcast.23), channel_id=1, source_target_pairs={{0,1},{1,0},{2,3},{3,2},{4,5},{5,4},{6,7},{7,6},{8,9},{9,8},{10,11... | collective-permute-start | bytes 3145736 | tf_op jit(solution)/shard_map/ppermute | solution.py:198
  61.2 14.3 %collective-permute-start.1 = (f32[32,4,64,128]{3,2,1,0:T(8,128)}, f32[32,4,64,128]{3,2,1,0:T(8,128)}, u32[]{:S(2)}, u32[]{:S(2)}) collective-permute-start(f32[32,4,64,128]{3,2,1,0:T(8,128)} %rotate.3), channel_id=1, source_target_pairs={{0,1},{1,0},{2,3},{3,2},{4,5},{5,4},{6,7},{7,6},{8,9},{9,8},{10,11... | collective-permute-start | bytes 12582920 | tf_op jit(solution)/shard_map/ppermute | solution.py:206
  79.3 15.3 %collective-permute-start.2 = (bf16[8,4,64,128]{3,2,1,0:T(8,128)(2,1)S(1)}, bf16[8,4,64,128]{3,2,1,0:T(8,128)(2,1)S(1)}, u32[]{:S(2)}, u32[]{:S(2)}) collective-permute-start(bf16[8,4,64,128]{3,2,1,0:T(8,128)(2,1)S(1)} %get-tuple-element.15), channel_id=1, source_target_pairs={{0,8},{1,3},{2,10},{3,5},{4,12},{5,7},{6,14},{7,1},{8,16},{9,11},{... | collective-permute-start | bytes 1572872 | tf_op jit(solution)/shard_map/ppermute | solution.py:210
  82.3 16.0 %collective-permute-start.4 = (bf16[8,4,64,128]{3,2,1,0:T(8,128)(2,1)S(1)}, bf16[8,4,64,128]{3,2,1,0:T(8,128)(2,1)S(1)}, u32[]{:S(2)}, u32[]{:S(2)}) collective-permute-start(bf16[8,4,64,128]{3,2,1,0:T(8,128)(2,1)S(1)} %get-tuple-element.16), channel_id=1, source_target_pairs={{0,24},{1,7},{2,26},{3,1},{4,28},{5,3},{6,30},{7,5},{8,0},{9,15},{... | collective-permute-start | bytes 1572872 | tf_op jit(solution)/shard_map/ppermute | solution.py:210
  82.3 16.0 %collective-permute-start.3 = (bf16[8,4,64,128]{3,2,1,0:T(8,128)(2,1)S(1)}, bf16[8,4,64,128]{3,2,1,0:T(8,128)(2,1)S(1)}, u32[]{:S(2)}, u32[]{:S(2)}) collective-permute-start(bf16[8,4,64,128]{3,2,1,0:T(8,128)(2,1)S(1)} %get-tuple-element.17), channel_id=1, source_target_pairs={{0,16},{1,5},{2,18},{3,7},{4,20},{5,1},{6,22},{7,3},{8,24},{9,13},... | collective-permute-start | bytes 1572872 | tf_op jit(solution)/shard_map/ppermute | solution.py:210
  98.7 7.7 %collective-permute-start.5 = (f32[2,4,64,128]{3,2,1,0:T(8,128)S(1)}, f32[2,4,64,128]{3,2,1,0:T(8,128)S(1)}, u32[]{:S(2)}, u32[]{:S(2)}) collective-permute-start(f32[2,4,64,128]{3,2,1,0:T(8,128)S(1)} %get-tuple-element.18), channel_id=1, source_target_pairs={{0,2},{1,9},{2,4},{3,11},{4,6},{5,13},{6,0},{7,15},{8,10},{9,17},{... | collective-permute-start | bytes 786440 | tf_op jit(solution)/shard_map/ppermute | solution.py:214
  98.8 9.9 %collective-permute-start.7 = (f32[2,4,64,128]{3,2,1,0:T(8,128)S(1)}, f32[2,4,64,128]{3,2,1,0:T(8,128)S(1)}, u32[]{:S(2)}, u32[]{:S(2)}) collective-permute-start(f32[2,4,64,128]{3,2,1,0:T(8,128)S(1)} %get-tuple-element.19), channel_id=1, source_target_pairs={{0,6},{1,25},{2,0},{3,27},{4,2},{5,29},{6,4},{7,31},{8,14},{9,1},{... | collective-permute-start | bytes 786440 | tf_op jit(solution)/shard_map/ppermute | solution.py:214
  102.0 7.9 %collective-permute-start.6 = (f32[2,4,64,128]{3,2,1,0:T(8,128)S(1)}, f32[2,4,64,128]{3,2,1,0:T(8,128)S(1)}, u32[]{:S(2)}, u32[]{:S(2)}) collective-permute-start(f32[2,4,64,128]{3,2,1,0:T(8,128)S(1)} %get-tuple-element.20), channel_id=1, source_target_pairs={{0,4},{1,17},{2,6},{3,19},{4,0},{5,21},{6,2},{7,23},{8,12},{9,25},... | collective-permute-start | bytes 786440 | tf_op jit(solution)/shard_map/ppermute | solution.py:214

commit v2 on v1

v2 whole, which is shorter than its diff:
```python
import functools
import math

import jax
import jax.numpy as jnp
from jax import lax
from jax.experimental import pallas as pl
from jax.experimental.pallas import tpu as pltpu
from jax.sharding import Mesh
from jax.sharding import PartitionSpec as P

GRID = 16
RMAX = 8
TWO_PI = 6.283185307179586
PLANE = ("y", "x", "c")
WHOLE = ("z", "y", "x", "c")
LINK = jnp.bfloat16
SIDE = 4
ROWS = 128


def owner_place(k, y, x, core):
    s1, s2 = (k // 8) % SIDE, (k // 2) % SIDE
    y_step = jnp.where(core == 0, s1, s2)
    x_step = jnp.where(core == 0, s2, s1)
    return (y + y_step) % SIDE, (x + x_step) % SIDE


def place_of(me):
    return me // 32, (me // 8) % SIDE, (me // 2) % SIDE, me % 2


def phase_matrix(me, coords, degeneracy, kpoints):
    count = coords.shape[1]
    z, y, x, c = place_of(me)
    at = lax.broadcasted_iota(jnp.int32, (64, 256), 0)
    core = (c + at // 32) % 2
    y_own, x_own = owner_place(at % 32, y, x, core)
    owned = z * 64 + (y_own * SIDE + x_own) * 4 + core * 2 + at % 2
    chosen = (lax.broadcasted_iota(jnp.int32, (64, 256), 1) == owned).astype(jnp.float32)
    turns = jnp.zeros((64, count), jnp.int32)
    for axis in range(3):
        line = kpoints[axis : axis + 1, :].astype(jnp.float32)
        k_axis = jnp.sum(chosen * line, axis=1, keepdims=True).astype(jnp.int32)
        turns = turns + k_axis * coords[axis : axis + 1, :]
    angles = (turns & (GRID - 1)).astype(jnp.float32) * (TWO_PI / GRID)
    weights = 1.0 / degeneracy.astype(jnp.float32)
    cosine = jnp.cos(angles) * weights
    sine = jnp.sin(angles) * weights
    along_x = coords[0:1, :].astype(jnp.float32) / RMAX
    rows = []
    for re, im in ((cosine, sine), (-along_x * sine, along_x * cosine)):
        for first, second in ((re, -im), (im, re)):
            pad = jnp.zeros((64, ROWS - count), jnp.float32)
            rows.append(jnp.concatenate([first, pad, second, pad], axis=1))
    return jnp.concatenate(rows, axis=0).astype(jnp.bfloat16)


def fourier_body(rows, me_ref, coords_ref, degen_ref, kpoints_ref, o_ref, f_ref, l_ref):
    @pl.when((pl.program_id(0) == 0) & (pl.program_id(1) == 0))
    def _():
        l_ref[...] = phase_matrix(me_ref[0], coords_ref[...], degen_ref[...], kpoints_ref[...])

    count = o_ref.shape[1]
    halves = []
    for part in range(2):
        block = o_ref[0, :, part]
        block = jnp.concatenate([block, jnp.zeros((ROWS - count, rows, 128), jnp.bfloat16)], axis=0)
        halves.append(jnp.swapaxes(block, 0, 1))
    stacked = jnp.concatenate(halves, axis=1)
    left = l_ref[...]
    sums = []
    for pair in range(rows // 2):
        right = jnp.concatenate([stacked[2 * pair], stacked[2 * pair + 1]], axis=1)
        both = jnp.dot(left, right, preferred_element_type=jnp.float32).astype(f_ref.dtype)
        sums += [both[:, :128], both[:, 128:]]
    f_ref[0] = jnp.swapaxes(jnp.stack(sums, axis=0), 0, 1)


def fourier(me, coords, degeneracy, kpoints, ops, rows=32):
    n_ops, count, _, width, _ = ops.shape
    lines = 256
    return pl.pallas_call(
        functools.partial(fourier_body, rows),
        grid_spec=pltpu.PrefetchScalarGridSpec(
            num_scalar_prefetch=1,
            grid=(n_ops, width // rows),
            in_specs=[
                pl.BlockSpec(coords.shape, lambda o, m, at: (0, 0)),
                pl.BlockSpec(degeneracy.shape, lambda o, m, at: (0, 0)),
                pl.BlockSpec(kpoints.shape, lambda o, m, at: (0, 0)),
                pl.BlockSpec((1, count, 2, rows, width), lambda o, m, at: (o, 0, 0, m, 0)),
            ],
            out_specs=pl.BlockSpec((1, lines, rows, width), lambda o, m, at: (o, 0, m, 0)),
            scratch_shapes=[pltpu.VMEM((lines, 2 * ROWS), jnp.bfloat16)],
        ),
        out_shape=jax.ShapeDtypeStruct((n_ops, lines, width, width), jnp.bfloat16),
        compiler_params=pltpu.CompilerParams(
            dimension_semantics=("arbitrary", "arbitrary"), vmem_limit_bytes=48 << 20
        ),
        cost_estimate=pl.CostEstimate(flops=8_000_000_000, bytes_accessed=33_000_000, transcendentals=0),
        name="fourier",
    )(me, coords, degeneracy, kpoints, ops)


def rotate_body(per_step, half, start, me_ref, v_ref, f_ref, b_ref):
    step = pl.program_id(0)
    _, y, x, c = place_of(me_ref[0])
    core = (c + half) % 2
    pairs, mids = [], []
    for j in range(per_step):
        k = start + step * per_step + j
        y_own, x_own = owner_place(k, y, x, core)
        where = (y_own * SIDE + x_own) * 2 + k % 2
        v_re, v_im = v_ref[where, 0], v_ref[where, 1]
        pairs.append((v_re, v_im))
        left = jnp.concatenate(
            [jnp.concatenate([v_re, v_im], axis=1), jnp.concatenate([-v_im, v_re], axis=1)], axis=0
        )
        found = []
        for o in range(2):
            right = jnp.concatenate(
                [jnp.concatenate([f_ref[o, 2 * p, j], f_ref[o, 2 * p + 1, j]], axis=0) for p in range(2)], axis=1
            )
            found.append(jnp.dot(left, right, preferred_element_type=jnp.float32))
        mids.append(found)
    for j in range(per_step):
        v_re, v_im = pairs[j]
        lines = []
        for o in range(2):
            for p in range(2):
                tile = mids[j][o][:, 128 * p : 128 * p + 128]
                lines.append(jnp.concatenate([tile[:64], tile[64:]], axis=1))
        mid = jnp.concatenate(lines, axis=0)
        high = mid.astype(jnp.bfloat16)
        low = (mid - high.astype(jnp.float32)).astype(jnp.bfloat16)
        right = jnp.concatenate(
            [jnp.concatenate([v_re, -v_im], axis=1), jnp.concatenate([v_im, v_re], axis=1)], axis=0
        )
        out = lax.dot_general(
            jnp.concatenate([high, low], axis=0),
            right,
            (((1,), (1,)), ((), ())),
            preferred_element_type=jnp.float32,
        )
        b_ref[j] = (out[:256] + out[256:]).reshape(4, 64, 128)


def rotate(me, vectors, sums, half, start, count, per_step=8):
    first = (half * 32 + start) // per_step
    return pl.pallas_call(
        functools.partial(rotate_body, per_step, half, start),
        grid_spec=pltpu.PrefetchScalarGridSpec(
            num_scalar_prefetch=1,
            grid=(count // per_step,),
            in_specs=[
                pl.BlockSpec(vectors.shape, lambda g, at: (0, 0, 0, 0)),
                pl.BlockSpec((2, 4, per_step, 128, 128), lambda g, at: (0, 0, first + g, 0, 0)),
            ],
            out_specs=pl.BlockSpec((per_step, 4, 64, 128), lambda g, at: (g, 0, 0, 0)),
        ),
        out_shape=jax.ShapeDtypeStruct((count, 4, 64, 128), jnp.float32),
        compiler_params=pltpu.CompilerParams(
            dimension_semantics=("arbitrary",), vmem_limit_bytes=48 << 20
        ),
        cost_estimate=pl.CostEstimate(flops=count * 120_000_000, bytes_accessed=count * 400_000, transcendentals=0),
        name="rotate",
    )(me, vectors, sums)


def final_body(b_ref, o_ref):
    factor = 1.0 / math.sqrt(64)
    high = lax.Precision.HIGHEST

    def wide(re, im):
        return jnp.concatenate(
            [jnp.concatenate([re, im], axis=1), jnp.concatenate([-im, re], axis=1)], axis=0
        )

    for k in range(b_ref.shape[0]):
        ham, deriv, posit, extra = (b_ref[k, j] for j in range(4))
        h_re, h_im = ham[:, :64], ham[:, 64:]
        d_re, d_im = deriv[:, :64], deriv[:, 64:]
        p_re, p_im = posit[:, :64], posit[:, 64:]
        one = jnp.dot(posit, wide(h_re - d_im, h_im + d_re), preferred_element_type=jnp.float32, precision=high)
        second = jnp.concatenate([h_re + d_im, h_im - d_re], axis=1)
        two = jnp.dot(second, wide(p_re, p_im), preferred_element_type=jnp.float32, precision=high)
        o_ref[k] = extra + factor * (one + two)


def final(bands):
    return pl.pallas_call(
        final_body,
        out_shape=jax.ShapeDtypeStruct((bands.shape[0], 64, 128), jnp.float32),
        name="final",
    )(bands)


def shift_pairs(stage, shift):
    pairs = []
    for z in range(4):
        for y in range(SIDE):
            for x in range(SIDE):
                for c in range(2):
                    along_y = (c == 0) == (stage == 0)
                    y_to, x_to = ((y + shift) % SIDE, x) if along_y else (y, (x + shift) % SIDE)
                    at = ((z * SIDE + y) * SIDE + x) * 2 + c
                    to = ((z * SIDE + y_to) * SIDE + x_to) * 2 + c
                    pairs.append((at, to))
    return pairs


def on_device(wannier_ops, r_coords, degeneracy, kpoints, bloch_vectors):
    me = lax.axis_index(WHOLE).astype(jnp.int32).reshape(1)
    slots = bloch_vectors.shape[0]
    swap = [(0, 1), (1, 0)]

    partner = lax.ppermute(bloch_vectors, "c", swap)
    copies = jnp.broadcast_to(partner[None], (SIDE * SIDE, *bloch_vectors.shape))
    theirs = lax.all_to_all(copies, ("y", "x"), 0, 0, tiled=True)
    theirs = theirs.reshape(SIDE * SIDE * slots, 2, 64, 128)
    sums = fourier(me, r_coords.T, degeneracy.reshape(1, -1), kpoints.T, wannier_ops)
    theirs, sums = lax.optimization_barrier((theirs, sums))
    mine = lax.ppermute(theirs, "c", swap)
    sums = sums.reshape(2, 4, 64, 128, 128)

    got = []
    for start in (0, 16):
        made = rotate(me, theirs, sums, 1, start, 16)
        got.append(lax.ppermute(made, "c", swap))
    own = rotate(me, mine, sums, 0, 0, 32).reshape(2, 2, -1, 4, 64, 128)
    parts = [own[s // 2, s % 2] + got[s // 2].reshape(2, -1, 4, 64, 128)[s % 2] for s in range(SIDE)]
    total = parts[0]
    for came in [lax.ppermute(parts[s].astype(LINK), WHOLE, shift_pairs(0, s)) for s in (2, 1, 3)]:
        total = total + came.astype(jnp.float32)
    parts = total.reshape(SIDE, slots, 4, 64, 128)
    total = parts[0]
    for came in [lax.ppermute(parts[s], WHOLE, shift_pairs(1, s)) for s in (2, 1, 3)]:
        total = total + came
    out = final(total)
    out = out.reshape(slots, 64, 2, 64)
    return jnp.transpose(out, (0, 2, 1, 3)).reshape(slots, 2, 64 * 64)


def solution(mesh):
    torus = Mesh(mesh.devices.reshape(4, 4, 4, 2), WHOLE)
    in_specs = (
        P(None, PLANE, None, None, None),
        P(PLANE, None),
        P(PLANE),
        P(),
        P(WHOLE, None, None, None),
    )
    return jax.shard_map(
        on_device, mesh=torus, in_specs=in_specs, out_specs=P(WHOLE, None, None), check_vma=False
    )
```

time: 116 us -> 87.1 us (0.75)
  Pallas kernels: 52.2 us -> 35.4 us
  other arithmetic: 7.84 us -> 1.92 us
  local copies, waits for them, and re-layouts: 7.25 us -> 3.01 us
  waiting for transfers between devices: 31.4 us -> 27.9 us
  starting transfers between devices: 15.5 us -> 17.8 us
    pallas_call x3 -> x4, Pallas kernels: 50.2 us -> 33.4 us  [the longest x1 19.5 us: fourier(): pl.pallas_call(functools.partial(fourier_body, rows), grid_spec=pltpu.Pre...]
    ppermute x2 -> x4, waiting for transfers between devices: 0.01 us -> 9.51 us  [the longest x1 8.05 us: on_device(): mine = lax.ppermute(theirs, 'c', swap)]
    all_to_all x1, waiting for transfers between devices: 9.09 us -> 0.01 us  [on_device(): theirs = lax.all_to_all(copies, ('y', 'x'), 0, 0, tiled=True)]
    another operation x6 -> x0, other arithmetic: 3.75 us -> none
    ppermute x3, waiting for transfers between devices: 14.5 us -> 11.6 us  [on_device(): lax.ppermute(parts[s].astype(LINK), WHOLE, shift_pairs(0, s))]
    ppermute x3, starting transfers between devices: 3.31 us -> 5.07 us  [on_device(): lax.ppermute(parts[s], WHOLE, shift_pairs(1, s))]
    div x2 -> x0, other arithmetic: 1.36 us -> none  [the longest x1 0.69 us: phase_matrix(): along_x = (coords[:, 0].astype(jnp.float32) / RMAX)[None, :]]
  transfers between devices with their start and end apart: 9 -> 11, of which waited for: 6 -> 7; matrix products, arithmetic and copies ran while one was open for 5% -> 0% of each run, Pallas kernels for 31% -> 30%
where the time goes in v2:
time: 87.1 us; the launch traced here: 86 us
  Pallas kernels  35.4 us (41%)
  waiting for transfers between devices  27.9 us (32%)
  starting transfers between devices  17.8 us (20%)
  local copies, waits for them, and re-layouts  3.01 us (3%)
  other arithmetic  1.92 us (2%)
    pallas_call x1, Pallas kernels, fourier(): pl.pallas_call(functools.partial(fourier_body, rows), grid_spec=pltpu.Pre...  19.5 us
    pallas_call x3, Pallas kernels, rotate(): pl.pallas_call(functools.partial(rotate_body, per_step, half, start), gri...  13.9 us
    ppermute x3, waiting for transfers between devices, on_device(): lax.ppermute(parts[s].astype(LINK), WHOLE, shift_pairs(0, s))  11.6 us
    ppermute x1, waiting for transfers between devices, on_device(): mine = lax.ppermute(theirs, 'c', swap)  8.05 us
    all_to_all x1, starting transfers between devices, on_device(): theirs = lax.all_to_all(copies, ('y', 'x'), 0, 0, tiled=True)  7.17 us
    ppermute x3, waiting for transfers between devices, on_device(): lax.ppermute(parts[s], WHOLE, shift_pairs(1, s))  6.72 us
    ppermute x3, starting transfers between devices, on_device(): lax.ppermute(parts[s], WHOLE, shift_pairs(1, s))  5.07 us
    ppermute x3, starting transfers between devices, on_device(): lax.ppermute(parts[s].astype(LINK), WHOLE, shift_pairs(0, s))  4.75 us
  transfers between devices with their start and end apart: 11, of which 7 were waited for; matrix products, arithmetic and copies ran while one was open for 0% of the time, Pallas kernels for 30%

profile of v2, /device:TPU:24, one launch (start us, length us, event | category | flops | bytes accessed | tf_op | source)
XLA Modules:
  0.0 86.0 jit_solution(16832101747125017405)
XLA Ops:
  0.0 0.0 copy-start
  0.0 0.0 copy-start.2
  0.0 0.0 copy-start.1
  0.0 0.1 collective-permute-start
  0.1 1.5 %collective-permute-done = bf16[2,2,64,128]{3,2,1,0:T(8,128)(2,1)S(1)} collective-permute-done((bf16[2,2,64,128]{3,2,1,0:T(8,128)(2,1)}, bf16[2,2,64,128]{3,2,1,0:T(8,128)(2,1)S(1)}, u32[]{:S(2)}, u32[]{:S(2)}) %collective-permute-start) | collective-permute-done | bytes 65568 | tf_op jit(solution)/shard_map/ppermute | solution.py:218
  1.6 1.2 %broadcast_in_dim.2 = bf16[16,2,2,64,128]{4,3,2,1,0:T(8,128)(2,1)} broadcast(bf16[2,2,64,128]{3,2,1,0:T(8,128)(2,1)S(1)} %collective-permute-done), dimensions={1,2,3,4} | broadcast | bytes 1114112 | tf_op jit(solution)/shard_map/broadcast_in_dim | solution.py:219
  2.8 7.2 %all-to-all-start = ((bf16[16,2,2,64,128]{4,3,2,1,0:T(8,128)(2,1)}), bf16[16,2,2,64,128]{4,3,2,1,0:T(8,128)(2,1)S(1)}, u32[]{:S(2)}, u32[]{:S(2)}) async-start(bf16[16,2,2,64,128]{4,3,2,1,0:T(8,128)(2,1)} %broadcast_in_dim.2), calls=%async_computation | async-start | bytes 2097152 | tf_op jit(solution)/shard_map/all_to_all | solution.py:220
  10.0 0.0 copy-done
  10.0 0.0 copy-done.2
  10.0 0.0 copy-done.1
  10.0 19.5 %fourier.1 = bf16[2,256,128,128]{3,2,1,0:T(8,128)(2,1)} custom-call(s32[1]{0:T(128)} %bitcast.me_ref, s32[3,125]{1,0:T(4,128)S(1)} %bitcast.32, s32[1,125]{1,0:T(1,128)S(1)} %bitcast.33, s32[3,256]{1,0:T(4,128)S(1)} %bitcast.31, bf16[2,125,2,128,128]{4,3,2,1,0:T(8,128)(2,1)} %o_ref.1), custom_call_target="tpu_custom_call" | custom-call | flops 8000000000 | bytes 33000000 | tf_op jit(solution)/shard_map/fourier/pallas_call | solution.py:83
  29.4 0.0 all-to-all-done
  29.5 3.7 %rotate.5 = f32[16,4,64,128]{3,2,1,0:T(8,128)S(1)} custom-call(s32[1]{0:T(128)} %bitcast.me_ref, bf16[32,2,64,128]{3,2,1,0:T(8,128)(2,1)S(1)} %bitcast.28, bf16[2,4,64,128,128]{4,3,2,1,0:T(8,128)(2,1)} %bitcast.34), custom_call_target="tpu_custom_call" | custom-call | flops 1920000000 | bytes 6400000 | tf_op jit(solution)/shard_map/rotate/pallas_call | solution.py:151
  33.2 3.7 %rotate.4 = f32[16,4,64,128]{3,2,1,0:T(8,128)S(1)} custom-call(s32[1]{0:T(128)} %bitcast.me_ref, bf16[32,2,64,128]{3,2,1,0:T(8,128)(2,1)S(1)} %bitcast.29, bf16[2,4,64,128,128]{4,3,2,1,0:T(8,128)(2,1)} %bitcast.35), custom_call_target="tpu_custom_call" | custom-call | flops 1920000000 | bytes 6400000 | tf_op jit(solution)/shard_map/rotate/pallas_call | solution.py:151
  36.9 0.1 collective-permute-start.2
  37.0 0.5 collective-permute-start.3
  37.5 0.1 collective-permute-start.1
  37.6 8.1 %collective-permute-done.1.v_ref = bf16[32,2,64,128]{3,2,1,0:T(8,128)(2,1)S(1)} collective-permute-done((bf16[32,2,64,128]{3,2,1,0:T(8,128)(2,1)S(1)}, bf16[32,2,64,128]{3,2,1,0:T(8,128)(2,1)S(1)}, u32[]{:S(2)}, u32[]{:S(2)}) %collective-permute-start.1) | collective-permute-done | bytes 1048608 | tf_op jit(solution)/shard_map/ppermute | solution.py:224
  45.6 6.5 %rotate.3 = f32[32,4,64,128]{3,2,1,0:T(8,128)S(1)} custom-call(s32[1]{0:T(128)} %bitcast.me_ref, bf16[32,2,64,128]{3,2,1,0:T(8,128)(2,1)S(1)} %collective-permute-done.1.v_ref, bf16[2,4,64,128,128]{4,3,2,1,0:T(8,128)(2,1)} %bitcast.36), custom_call_target="tpu_custom_call" | custom-call | flops 3840000000 | bytes 12800000 | tf_op jit(solution)/shard_map/rotate/pallas_call | solution.py:151
  52.1 0.0 collective-permute-done.2
  52.1 0.0 collective-permute-done.3
  52.1 0.7 fusion.2
  52.9 1.5 %collective-permute-start.4 = (bf16[8,4,64,128]{3,2,1,0:T(8,128)(2,1)S(1)}, bf16[8,4,64,128]{3,2,1,0:T(8,128)(2,1)S(1)}, u32[]{:S(2)}, u32[]{:S(2)}) collective-permute-start(bf16[8,4,64,128]{3,2,1,0:T(8,128)(2,1)S(1)} %get-tuple-element.9), channel_id=1, source_target_pairs={{0,16},{1,5},{2,18},{3,7},{4,20},{5,1},{6,22},{7,3},{8,24},{9,13},... | collective-permute-start | bytes 1572872 | tf_op jit(solution)/shard_map/ppermute | solution.py:234
  54.4 0.0 collective-permute-start.6
  54.4 3.2 %collective-permute-start.5 = (bf16[8,4,64,128]{3,2,1,0:T(8,128)(2,1)S(1)}, bf16[8,4,64,128]{3,2,1,0:T(8,128)(2,1)S(1)}, u32[]{:S(2)}, u32[]{:S(2)}) collective-permute-start(bf16[8,4,64,128]{3,2,1,0:T(8,128)(2,1)S(1)} %get-tuple-element.11), channel_id=1, source_target_pairs={{0,8},{1,3},{2,10},{3,5},{4,12},{5,7},{6,14},{7,1},{8,16},{9,11},{... | collective-permute-start | bytes 1572872 | tf_op jit(solution)/shard_map/ppermute | solution.py:234
  57.6 6.1 %collective-permute-done.4 = bf16[8,4,64,128]{3,2,1,0:T(8,128)(2,1)S(1)} collective-permute-done((bf16[8,4,64,128]{3,2,1,0:T(8,128)(2,1)S(1)}, bf16[8,4,64,128]{3,2,1,0:T(8,128)(2,1)S(1)}, u32[]{:S(2)}, u32[]{:S(2)}) %collective-permute-start.4) | collective-permute-done | bytes 524320 | tf_op jit(solution)/shard_map/ppermute | solution.py:234
  63.7 5.5 %collective-permute-done.6 = bf16[8,4,64,128]{3,2,1,0:T(8,128)(2,1)S(1)} collective-permute-done((bf16[8,4,64,128]{3,2,1,0:T(8,128)(2,1)S(1)}, bf16[8,4,64,128]{3,2,1,0:T(8,128)(2,1)S(1)}, u32[]{:S(2)}, u32[]{:S(2)}) %collective-permute-start.6) | collective-permute-done | bytes 524320 | tf_op jit(solution)/shard_map/ppermute | solution.py:234
  69.3 0.0 collective-permute-done.5
  69.3 0.4 fusion.5
  69.7 0.1 fusion.8
  69.7 3.0 %collective-permute-start.7 = (f32[2,4,64,128]{3,2,1,0:T(8,128)S(1)}, f32[2,4,64,128]{3,2,1,0:T(8,128)S(1)}, u32[]{:S(2)}, u32[]{:S(2)}) collective-permute-start(f32[2,4,64,128]{3,2,1,0:T(8,128)S(1)} %get-tuple-element.12), channel_id=1, source_target_pairs={{0,4},{1,17},{2,6},{3,19},{4,0},{5,21},{6,2},{7,23},{8,12},{9,25},... | collective-permute-start | bytes 786440 | tf_op jit(solution)/shard_map/ppermute | solution.py:238
  72.8 1.2 %collective-permute-start.9 = (f32[2,4,64,128]{3,2,1,0:T(8,128)S(1)}, f32[2,4,64,128]{3,2,1,0:T(8,128)S(1)}, u32[]{:S(2)}, u32[]{:S(2)}) collective-permute-start(f32[2,4,64,128]{3,2,1,0:T(8,128)S(1)} %get-tuple-element.13), channel_id=1, source_target_pairs={{0,6},{1,25},{2,0},{3,27},{4,2},{5,29},{6,4},{7,31},{8,14},{9,1},{... | collective-permute-start | bytes 786440 | tf_op jit(solution)/shard_map/ppermute | solution.py:238
  74.0 0.9 %collective-permute-start.8 = (f32[2,4,64,128]{3,2,1,0:T(8,128)S(1)}, f32[2,4,64,128]{3,2,1,0:T(8,128)S(1)}, u32[]{:S(2)}, u32[]{:S(2)}) collective-permute-start(f32[2,4,64,128]{3,2,1,0:T(8,128)S(1)} %get-tuple-element.14), channel_id=1, source_target_pairs={{0,2},{1,9},{2,4},{3,11},{4,6},{5,13},{6,0},{7,15},{8,10},{9,17},{... | collective-permute-start | bytes 786440 | tf_op jit(solution)/shard_map/ppermute | solution.py:238
  74.8 2.9 %collective-permute-done.7 = f32[2,4,64,128]{3,2,1,0:T(8,128)S(1)} collective-permute-done((f32[2,4,64,128]{3,2,1,0:T(8,128)S(1)}, f32[2,4,64,128]{3,2,1,0:T(8,128)S(1)}, u32[]{:S(2)}, u32[]{:S(2)}) %collective-permute-start.7) | collective-permute-done | bytes 262176 | tf_op jit(solution)/shard_map/ppermute | solution.py:238
  77.7 2.8 %collective-permute-done.9 = f32[2,4,64,128]{3,2,1,0:T(8,128)S(1)} collective-permute-done((f32[2,4,64,128]{3,2,1,0:T(8,128)S(1)}, f32[2,4,64,128]{3,2,1,0:T(8,128)S(1)}, u32[]{:S(2)}, u32[]{:S(2)}) %collective-permute-start.9) | collective-permute-done | bytes 262176 | tf_op jit(solution)/shard_map/ppermute | solution.py:238
  80.5 1.0 %collective-permute-done.8 = f32[2,4,64,128]{3,2,1,0:T(8,128)S(1)} collective-permute-done((f32[2,4,64,128]{3,2,1,0:T(8,128)S(1)}, f32[2,4,64,128]{3,2,1,0:T(8,128)S(1)}, u32[]{:S(2)}, u32[]{:S(2)}) %collective-permute-start.8) | collective-permute-done | bytes 262176 | tf_op jit(solution)/shard_map/ppermute | solution.py:238
  81.5 0.8 fusion.7.b_ref
  82.3 2.0 %final.1 = f32[2,64,128]{2,1,0:T(8,128)} custom-call(f32[2,4,64,128]{3,2,1,0:T(8,128)} %fusion.7.b_ref), custom_call_target="tpu_custom_call" | custom-call | tf_op jit(solution)/shard_map/final/pallas_call | solution.py:192
  84.3 1.0 %reshape.48 = f32[2,64,2,64]{3,2,1,0:T(2,128)S(1)} reshape(f32[2,64,128]{2,1,0:T(8,128)} %final.1) | data formatting | bytes 131072 | tf_op jit(solution)/shard_map/reshape | solution.py:241
  85.3 0.7 reshape.49
  (1 shorter events, 0.0 us)
Async XLA Ops:
  0.0 10.0 %copy-start = (s32[256,3]{0,1:T(4,128)S(1)}, s32[256,3]{0,1:T(4,128)}, u32[]{:S(2)}) copy-start(s32[256,3]{0,1:T(4,128)} %param.8) | copy-start | bytes 9220
  0.0 10.0 %copy-start.2 = (s32[125]{0:T(128)S(1)}, s32[125]{0:T(128)}, u32[]{:S(2)}) copy-start(s32[125]{0:T(128)} %param.7) | copy-start | bytes 1504
  0.0 10.0 %copy-start.1 = (s32[125,3]{0,1:T(4,128)S(1)}, s32[125,3]{0,1:T(4,128)}, u32[]{:S(2)}) copy-start(s32[125,3]{0,1:T(4,128)} %param.6) | copy-start | bytes 4504
  0.0 1.5 %collective-permute-start = (bf16[2,2,64,128]{3,2,1,0:T(8,128)(2,1)}, bf16[2,2,64,128]{3,2,1,0:T(8,128)(2,1)S(1)}, u32[]{:S(2)}, u32[]{:S(2)}) collective-permute-start(bf16[2,2,64,128]{3,2,1,0:T(8,128)(2,1)} %param.9), channel_id=1, source_target_pairs={{0,1},{1,0},{2,3},{3,2},{4,5},{5,4},{6,7},{7,6},{8,9},{9,8},{10,11... | collective-permute-start | bytes 196616 | tf_op jit(solution)/shard_map/ppermute | solution.py:218
  2.8 26.7 %all-to-all-start = ((bf16[16,2,2,64,128]{4,3,2,1,0:T(8,128)(2,1)}), bf16[16,2,2,64,128]{4,3,2,1,0:T(8,128)(2,1)S(1)}, u32[]{:S(2)}, u32[]{:S(2)}) async-start(bf16[16,2,2,64,128]{4,3,2,1,0:T(8,128)(2,1)} %broadcast_in_dim.2), calls=%async_computation | async-start | bytes 2097152 | tf_op jit(solution)/shard_map/all_to_all | solution.py:220
  36.9 15.2 %collective-permute-start.2 = (f32[16,4,64,128]{3,2,1,0:T(8,128)S(1)}, f32[16,4,64,128]{3,2,1,0:T(8,128)S(1)}, u32[]{:S(2)}, u32[]{:S(2)}) collective-permute-start(f32[16,4,64,128]{3,2,1,0:T(8,128)S(1)} %rotate.4), channel_id=1, source_target_pairs={{0,1},{1,0},{2,3},{3,2},{4,5},{5,4},{6,7},{7,6},{8,9},{9,8},{10,11... | collective-permute-start | bytes 6291464 | tf_op jit(solution)/shard_map/ppermute | solution.py:230
  37.0 15.1 %collective-permute-start.3 = (f32[16,4,64,128]{3,2,1,0:T(8,128)S(1)}, f32[16,4,64,128]{3,2,1,0:T(8,128)S(1)}, u32[]{:S(2)}, u32[]{:S(2)}) collective-permute-start(f32[16,4,64,128]{3,2,1,0:T(8,128)S(1)} %rotate.5), channel_id=1, source_target_pairs={{0,1},{1,0},{2,3},{3,2},{4,5},{5,4},{6,7},{7,6},{8,9},{9,8},{10,11... | collective-permute-start | bytes 6291464 | tf_op jit(solution)/shard_map/ppermute | solution.py:230
  37.5 8.1 %collective-permute-start.1 = (bf16[32,2,64,128]{3,2,1,0:T(8,128)(2,1)S(1)}, bf16[32,2,64,128]{3,2,1,0:T(8,128)(2,1)S(1)}, u32[]{:S(2)}, u32[]{:S(2)}) collective-permute-start(bf16[32,2,64,128]{3,2,1,0:T(8,128)(2,1)S(1)} %bitcast.30), channel_id=1, source_target_pairs={{0,1},{1,0},{2,3},{3,2},{4,5},{5,4},{6,7},{7,6},{8,9},{9,8},{10,11... | collective-permute-start | bytes 3145736 | tf_op jit(solution)/shard_map/ppermute | solution.py:224
  52.9 10.9 %collective-permute-start.4 = (bf16[8,4,64,128]{3,2,1,0:T(8,128)(2,1)S(1)}, bf16[8,4,64,128]{3,2,1,0:T(8,128)(2,1)S(1)}, u32[]{:S(2)}, u32[]{:S(2)}) collective-permute-start(bf16[8,4,64,128]{3,2,1,0:T(8,128)(2,1)S(1)} %get-tuple-element.9), channel_id=1, source_target_pairs={{0,16},{1,5},{2,18},{3,7},{4,20},{5,1},{6,22},{7,3},{8,24},{9,13},... | collective-permute-start | bytes 1572872 | tf_op jit(solution)/shard_map/ppermute | solution.py:234
  54.4 14.9 %collective-permute-start.6 = (bf16[8,4,64,128]{3,2,1,0:T(8,128)(2,1)S(1)}, bf16[8,4,64,128]{3,2,1,0:T(8,128)(2,1)S(1)}, u32[]{:S(2)}, u32[]{:S(2)}) collective-permute-start(bf16[8,4,64,128]{3,2,1,0:T(8,128)(2,1)S(1)} %get-tuple-element.10), channel_id=1, source_target_pairs={{0,24},{1,7},{2,26},{3,1},{4,28},{5,3},{6,30},{7,5},{8,0},{9,15},{... | collective-permute-start | bytes 1572872 | tf_op jit(solution)/shard_map/ppermute | solution.py:234
  54.4 14.9 %collective-permute-start.5 = (bf16[8,4,64,128]{3,2,1,0:T(8,128)(2,1)S(1)}, bf16[8,4,64,128]{3,2,1,0:T(8,128)(2,1)S(1)}, u32[]{:S(2)}, u32[]{:S(2)}) collective-permute-start(bf16[8,4,64,128]{3,2,1,0:T(8,128)(2,1)S(1)} %get-tuple-element.11), channel_id=1, source_target_pairs={{0,8},{1,3},{2,10},{3,5},{4,12},{5,7},{6,14},{7,1},{8,16},{9,11},{... | collective-permute-start | bytes 1572872 | tf_op jit(solution)/shard_map/ppermute | solution.py:234
  69.7 8.0 %collective-permute-start.7 = (f32[2,4,64,128]{3,2,1,0:T(8,128)S(1)}, f32[2,4,64,128]{3,2,1,0:T(8,128)S(1)}, u32[]{:S(2)}, u32[]{:S(2)}) collective-permute-start(f32[2,4,64,128]{3,2,1,0:T(8,128)S(1)} %get-tuple-element.12), channel_id=1, source_target_pairs={{0,4},{1,17},{2,6},{3,19},{4,0},{5,21},{6,2},{7,23},{8,12},{9,25},... | collective-permute-start | bytes 786440 | tf_op jit(solution)/shard_map/ppermute | solution.py:238
  72.8 7.7 %collective-permute-start.9 = (f32[2,4,64,128]{3,2,1,0:T(8,128)S(1)}, f32[2,4,64,128]{3,2,1,0:T(8,128)S(1)}, u32[]{:S(2)}, u32[]{:S(2)}) collective-permute-start(f32[2,4,64,128]{3,2,1,0:T(8,128)S(1)} %get-tuple-element.13), channel_id=1, source_target_pairs={{0,6},{1,25},{2,0},{3,27},{4,2},{5,29},{6,4},{7,31},{8,14},{9,1},{... | collective-permute-start | bytes 786440 | tf_op jit(solution)/shard_map/ppermute | solution.py:238
  74.0 7.6 %collective-permute-start.8 = (f32[2,4,64,128]{3,2,1,0:T(8,128)S(1)}, f32[2,4,64,128]{3,2,1,0:T(8,128)S(1)}, u32[]{:S(2)}, u32[]{:S(2)}) collective-permute-start(f32[2,4,64,128]{3,2,1,0:T(8,128)S(1)} %get-tuple-element.14), channel_id=1, source_target_pairs={{0,2},{1,9},{2,4},{3,11},{4,6},{5,13},{6,0},{7,15},{8,10},{9,17},{... | collective-permute-start | bytes 786440 | tf_op jit(solution)/shard_map/ppermute | solution.py:238
